TPU v7x, 32 devices: a whole 2x2x4 slice. The times are simulated.
32 devices in a mesh: fsdp: 32 (over z, y, x, core).
Axes of the slice: x: 2, y: 2, z: 4, core: 2. Of those that a mesh axis runs over, the one named last changes fastest.
Arguments:
- tokens: int32 [32, 256], P('fsdp')
- embed_table: float32 [32000, 2048], P('fsdp')
- norm_gain: float32 [2048], P('fsdp')
- w_query: float32 [2048, 2048], P('fsdp')
- w_key: float32 [2048, 256], P('fsdp')
- w_value: float32 [2048, 256], P('fsdp')
- d_query: bfloat16 [32, 256, 2048], P('fsdp')
- d_key: bfloat16 [32, 256, 256], P('fsdp')
- d_value: bfloat16 [32, 256, 256], P('fsdp')
Outputs:
- output 1: bfloat16 [32, 256, 2048], P('fsdp')
- output 2: bfloat16 [32, 256, 256], P('fsdp')
- output 3: bfloat16 [32, 256, 256], P('fsdp')
- output 4: float32 [32000, 2048], P('fsdp')
- output 5: float32 [2048], P('fsdp')
- output 6: float32 [2048, 2048], P('fsdp')
- output 7: float32 [2048, 256], P('fsdp')
- output 8: float32 [2048, 256], P('fsdp')
All inputs are finite; a program needn't handle non-finite values.
Results may differ from a plain program's by a relative error of at most 0.00411384.
Values are sent between devices in bfloat16 or wider.
A program may use at most 1 GiB of HBM per device.

v0:
```python
import jax
import jax.numpy as jnp
from jax import lax
from jax.sharding import PartitionSpec as P

AXIS_NAME = "fsdp"


def norm_forward(x_rows, gain_full):
    inv_rms = lax.rsqrt(jnp.mean(x_rows * x_rows, axis=-1, keepdims=True) + 1e-5)
    h_rows = x_rows * inv_rms
    return inv_rms, h_rows, (h_rows * gain_full).astype(jnp.bfloat16)


def solution(mesh):
    def local_step(tokens, embed_shard, gain_shard, wq_shard, wk_shard, wv_shard, d_query, d_key, d_value):
        vocab_local = embed_shard.shape[0]
        dev_index = lax.axis_index(AXIS_NAME)
        all_tokens = lax.all_gather(tokens, AXIS_NAME, axis=0, tiled=True)
        local_ids = all_tokens - dev_index * vocab_local
        is_owned = (local_ids >= 0) & (local_ids < vocab_local)
        owned_rows = jnp.take(embed_shard, jnp.where(is_owned, local_ids, 0), axis=0).astype(jnp.bfloat16)
        part_rows = jnp.where(is_owned[:, :, None], owned_rows, jnp.zeros((), jnp.bfloat16))
        x_rows = lax.psum_scatter(part_rows, AXIS_NAME, scatter_dimension=0, tiled=True).astype(jnp.float32)
        gain_full = lax.all_gather(gain_shard, AXIS_NAME, axis=0, tiled=True)
        wq_full = lax.all_gather(wq_shard.astype(jnp.bfloat16), AXIS_NAME, axis=0, tiled=True)
        wk_full = lax.all_gather(wk_shard.astype(jnp.bfloat16), AXIS_NAME, axis=0, tiled=True)
        wv_full = lax.all_gather(wv_shard.astype(jnp.bfloat16), AXIS_NAME, axis=0, tiled=True)
        inv_rms, h_rows, normed = norm_forward(x_rows, gain_full)
        query_proj = jnp.einsum("bsd,df->bsf", normed, wq_full, preferred_element_type=jnp.float32).astype(jnp.bfloat16)
        key_proj = jnp.einsum("bsd,df->bsf", normed, wk_full, preferred_element_type=jnp.float32).astype(jnp.bfloat16)
        value_proj = jnp.einsum("bsd,df->bsf", normed, wv_full, preferred_element_type=jnp.float32).astype(jnp.bfloat16)
        d_w_query = lax.psum_scatter(jnp.einsum("bsd,bsf->df", normed, d_query, preferred_element_type=jnp.float32), AXIS_NAME, scatter_dimension=0, tiled=True)
        d_w_key = lax.psum_scatter(jnp.einsum("bsd,bsf->df", normed, d_key, preferred_element_type=jnp.float32), AXIS_NAME, scatter_dimension=0, tiled=True)
        d_w_value = lax.psum_scatter(jnp.einsum("bsd,bsf->df", normed, d_value, preferred_element_type=jnp.float32), AXIS_NAME, scatter_dimension=0, tiled=True)
        d_normed = (jnp.einsum("bsf,df->bsd", d_query, wq_full, preferred_element_type=jnp.float32)
                    + jnp.einsum("bsf,df->bsd", d_key, wk_full, preferred_element_type=jnp.float32)
                    + jnp.einsum("bsf,df->bsd", d_value, wv_full, preferred_element_type=jnp.float32))
        d_norm_gain = lax.psum_scatter(jnp.sum(d_normed * h_rows, axis=(0, 1)), AXIS_NAME, scatter_dimension=0, tiled=True)
        u_rows = d_normed * gain_full
        d_x = inv_rms * (u_rows - h_rows * jnp.mean(u_rows * h_rows, axis=-1, keepdims=True))
        all_dx = lax.all_gather(d_x, AXIS_NAME, axis=0, tiled=True)
        scatter_ids = jnp.where(is_owned, local_ids, vocab_local)
        d_embed = jnp.zeros(embed_shard.shape, jnp.float32).at[scatter_ids].add(all_dx, mode="drop")
        return (query_proj, key_proj, value_proj, d_embed, d_norm_gain, d_w_query, d_w_key, d_w_value)

    row_spec = P(AXIS_NAME, None)
    act_spec = P(AXIS_NAME, None, None)
    vec_spec = P(AXIS_NAME)
    return jax.shard_map(local_step, mesh=mesh,
                         in_specs=(row_spec, row_spec, vec_spec, row_spec, row_spec, row_spec, act_spec, act_spec, act_spec),
                         out_specs=(act_spec, act_spec, act_spec, row_spec, vec_spec, row_spec, row_spec, row_spec),
                         check_vma=False)
```

profile of v0, /device:TPU:0, one launch (start us, length us, event | category | flops | bytes accessed | tf_op | source)
XLA Modules:
  0.0 1392.7 jit_solution(7700663610178207622)
XLA Ops:
  7.2 1.9 convert_element_type.39
  9.1 0.0 all-gather.8.cloned.1.call-start
  9.2 1.5 convert_element_type.42
  10.6 0.0 reduce-scatter.5.cloned.1.call-start
  10.7 43.4 %all-gather = s32[32,1,256]{2,1,0:T(1,128)S(1)} all-gather(s32[1,1,256]{2,1,0:T(1,128)} %bitcast.82), channel_id=1, replica_groups=mesh['fsdp'=32] {'fsdp'}, dimensions={0}, use_global_device_ids=true | all-gather | bytes 33792 | tf_op jit(solution)/shard_map/all_gather | solution.py:19
  54.2 64.7 %gather_fusion = bf16[8192,2048]{1,0:T(8,128)(2,1)} fusion(f32[1000,2048]{1,0:T(8,128)} %param.10, s32[8192]{0:T(1024)S(1)} %broadcast_clamp_fusion), kind=kCustom, calls=%fused_computation | custom fusion | bytes 67141632 | tf_op jit(solution)/shard_map/jit(_take)/gather | solution.py:22
  118.9 22.8 %fusion = bf16[32,256,2048]{2,1,0:T(8,128)(2,1)} fusion(bf16[32,256,2048]{2,1,0:T(8,128)(2,1)} %bitcast.76, pred[32,256]{1,0:T(8,128)(4,1)S(1)} %get-tuple-element.13, pred[32,256]{1,0:T(8,128)(4,1)S(1)} %get-tuple-element.12), kind=kLoop, calls=%fused_computation.3 | loop fusion | flops 33554432 | bytes 67125248 | tf_op jit(solution)/shard_map/jit(_where)/select_n | solution.py:23
  141.7 0.8 copy-done.6
  142.5 0.6 convert_element_type.45
  143.2 0.3 dynamic-update-slice
  143.5 43.8 %all-reduce = f32[2048]{0:T(1024)S(1)} all-reduce(f32[2048]{0:T(1024)S(1)} %dynamic-update-slice), channel_id=1, replica_groups=mesh['fsdp'=32] {'fsdp'}, use_global_device_ids=true, to_apply=%add | all-reduce | flops 2048 | bytes 16384
  187.3 5.8 fusion.19
  193.1 3.0 convolution_add_fusion.1
  196.2 307.5 %reduce-scatter.5.cloned.1.call-done = bf16[1,256,2048]{2,1,0:T(8,128)(2,1)} async-done(((bf16[32,256,2048]{2,1,0:T(8,128)(2,1)}), bf16[1,256,2048]{2,1,0:T(8,128)(2,1)}) %reduce-scatter.5.cloned.1.call-update) | async-done | bytes 1048592 | tf_op jit(solution)/shard_map/reduce_scatter | solution.py:24
  503.6 1.5 fusion.13
  505.2 62.8 %all-gather.10.cloned.1.call-done = bf16[2048,256]{1,0:T(8,128)(2,1)} async-done(((bf16[64,256]{1,0:T(8,128)(2,1)}), bf16[2048,256]{1,0:T(8,128)(2,1)}) %all-gather.10.cloned.1.call-update) | async-done | bytes 1048592 | tf_op jit(solution)/shard_map/all_gather | solution.py:28
  568.0 3.1 fusion.12
  571.1 1.8 fusion.11
  573.0 1.9 fusion.24
  575.0 1.9 fusion.21
  576.9 0.0 reduce-scatter.7.cloned.1.call-start
  577.0 8.3 fusion.17
  585.3 42.1 %all-reduce.1 = f32[2048]{0:T(1024)S(1)} all-reduce(f32[2048]{0:T(1024)S(1)} %get-tuple-element.8), channel_id=3, replica_groups=mesh['fsdp'=32] {'fsdp'}, use_global_device_ids=true, to_apply=%region_5.6.clone | all-reduce | flops 2048 | bytes 16384
  627.4 0.6 dynamic-slice
  628.0 1.2 fusion.14
  629.2 1.1 fusion.15
  630.3 6.7 fusion.7
  637.1 291.0 %all-gather.12.cloned.1.call-done = f32[32,256,2048]{2,1,0:T(8,128)} async-done(((f32[1,256,2048]{2,1,0:T(8,128)}), f32[32,256,2048]{2,1,0:T(8,128)}) %all-gather.12.cloned.1.call-update) | async-done | bytes 67108880 | tf_op jit(solution)/shard_map/all_gather | solution.py:42
  928.1 105.6 %scatter_custom_fusion = f32[1000,2048]{1,0:T(8,128)} fusion(s32[8192]{0:T(1024)S(1)} %bitcast.81, f32[8192,2048]{1,0:T(8,128)} %bitcast.10, f32[]{:T(128)} %constant.15.clone.1), kind=kCustom, calls=%fused_computation.4 | custom fusion | flops 16777216 | bytes 8192512 | tf_op jit(solution)/shard_map/scatter-add | solution.py:44
  1033.7 34.0 %reduce-scatter.9.cloned.1.call-done = f32[64,256]{1,0:T(8,128)} async-done(((f32[2048,256]{1,0:T(8,128)}), f32[64,256]{1,0:T(8,128)}) %reduce-scatter.9.cloned.1.call-update) | async-done | bytes 65552 | tf_op jit(solution)/shard_map/reduce_scatter | solution.py:34
  1067.7 136.7 %reduce-scatter.11.cloned.1.call-done = f32[64,256]{1,0:T(8,128)} async-done(((f32[2048,256]{1,0:T(8,128)}), f32[64,256]{1,0:T(8,128)}) %reduce-scatter.11.cloned.1.call-update) | async-done | bytes 65552 | tf_op jit(solution)/shard_map/reduce_scatter | solution.py:35
  1204.4 181.5 %reduce-scatter.7.cloned.1.call-done = f32[64,2048]{1,0:T(8,128)} async-done(((f32[2048,2048]{1,0:T(8,128)}), f32[64,2048]{1,0:T(8,128)}) %reduce-scatter.7.cloned.1.call-update) | async-done | bytes 524304 | tf_op jit(solution)/shard_map/reduce_scatter | solution.py:33
  (39 shorter events, 0.5 us)
Async XLA Ops:
  7.2 180.1 %copy-start = (bf16[1,256,2048]{2,1,0:T(8,128)(2,1)S(1)}, bf16[1,256,2048]{2,1,0:T(8,128)(2,1)}, u32[]{:S(2)}) copy-start(bf16[1,256,2048]{2,1,0:T(8,128)(2,1)} %param.15) | copy-start | bytes 3145732
  7.2 180.1 %all-gather.6.cloned.1.call-start = ((), (), s32[]{:S(2)}) async-start(), calls=%async_computation.5 | async-start | bytes 8650752 | tf_op jit(solution)/shard_map/all_gather | solution.py:26
  9.1 184.0 %all-gather.8.cloned.1.call-start = ((), (), s32[]{:S(2)}) async-start(), calls=%async_computation.6 | async-start | bytes 1081344 | tf_op jit(solution)/shard_map/all_gather | solution.py:27
  10.6 493.0 %reduce-scatter.5.cloned.1.call-start = ((), (), s32[]{:S(2)}) async-start(), calls=%async_computation.4 | async-start | bytes 34603008 | tf_op jit(solution)/shard_map/reduce_scatter | solution.py:24
  141.6 0.8 copy-start.6
  141.6 1.6 copy-start.7
  141.7 426.3 %all-gather.10.cloned.1.call-start = ((), (), s32[]{:S(2)}) async-start(), calls=%async_computation.7 | async-start | bytes 1081344 | tf_op jit(solution)/shard_map/all_gather | solution.py:28
  143.1 784.9 %all-gather.12.cloned.1.call-start = ((), (), s32[]{:S(2)}) async-start(), calls=%async_computation.8 | async-start | bytes 69206016 | tf_op jit(solution)/shard_map/all_gather | solution.py:42
  187.3 5.8 copy-start.5
  193.1 374.9 %copy-start.4 = (bf16[1,256,256]{2,1,0:T(8,128)(2,1)S(1)}, bf16[1,256,256]{2,1,0:T(8,128)(2,1)}, u32[]{:S(2)}) copy-start(bf16[1,256,256]{2,1,0:T(8,128)(2,1)} %param.17) | copy-start | bytes 393220
  505.2 65.9 %copy-start.1 = (bf16[1,256,2048]{2,1,0:T(8,128)(2,1)S(1)}, bf16[1,256,2048]{2,1,0:T(8,128)(2,1)}, u32[]{:S(2)}) copy-start(bf16[1,256,2048]{2,1,0:T(8,128)(2,1)} %reduce-scatter.5.cloned.1.call-done) | copy-start | bytes 3145732
  572.9 494.7 %reduce-scatter.9.cloned.1.call-start = ((), (), s32[]{:S(2)}) async-start(), calls=%async_computation.10 | async-start | bytes 2162688 | tf_op jit(solution)/shard_map/reduce_scatter | solution.py:34
  574.9 629.5 %reduce-scatter.11.cloned.1.call-start = ((), (), s32[]{:S(2)}) async-start(), calls=%async_computation.11 | async-start | bytes 2162688 | tf_op jit(solution)/shard_map/reduce_scatter | solution.py:35
  576.9 808.9 %reduce-scatter.7.cloned.1.call-start = ((), (), s32[]{:S(2)}) async-start(), calls=%async_computation.9 | async-start | bytes 17301504 | tf_op jit(solution)/shard_map/reduce_scatter | solution.py:33
  585.3 42.8 %copy-start.2 = (bf16[2048,256]{1,0:T(8,128)(2,1)S(1)}, bf16[2048,256]{1,0:T(8,128)(2,1)}, u32[]{:S(2)}) copy-start(bf16[2048,256]{1,0:T(8,128)(2,1)} %all-gather.8.cloned.1.call-done) | copy-start | bytes 3145732
  627.4 1.7 copy-start.3
Sparse Core Ops, SparseCore 0:
  11.4 79.7 all-gather.5
  94.7 52.4 all-gather.7
  149.5 354.1 reduce-scatter.4
  506.9 60.9 all-gather.9
  573.0 354.9 all-gather.11
  930.7 136.8 reduce-scatter.8
  1070.5 133.8 reduce-scatter.10
  1207.3 178.5 reduce-scatter.6
where the time goes:
time: 1390 us
  waiting for transfers between devices  1010 us (73%)
  other arithmetic  136 us (10%)
  blocking collectives  129 us (9%)
  local copies, waits for them, and re-layouts  66.4 us (5%)
  matrix products  33.1 us (2%)
  between operations  14.3 us (1%)
    reduce_scatter x1, waiting for transfers between devices, local_step(): lax.psum_scatter(part_rows, AXIS_NAME, scatter_dimension=0, tiled=True)  307 us
    all_gather x1, waiting for transfers between devices, local_step(): all_dx = lax.all_gather(d_x, AXIS_NAME, axis=0, tiled=True)  291 us
    reduce_scatter x1, waiting for transfers between devices, local_step(): lax.psum_scatter(jnp.einsum('bsd,bsf->df', normed, d_query, preferred_ele...  182 us
    reduce_scatter x1, waiting for transfers between devices, local_step(): lax.psum_scatter(jnp.einsum('bsd,bsf->df', normed, d_value, preferred_ele...  137 us
    scatter-add x1, other arithmetic, local_step(): jnp.zeros(embed_shard.shape, jnp.float32).at[scatter_ids]  106 us
    unnamed x2, blocking collectives  85.9 us
    gather x1, local copies, waits for them, and re-layouts, local_step(): jnp.take(embed_shard, jnp.where(is_owned, local_ids, 0), axis=0)  64.7 us
    all_gather x1, waiting for transfers between devices, local_step(): lax.all_gather(wv_shard.astype(jnp.bfloat16), AXIS_NAME, axis=0, tiled=True)  62.8 us
  transfers between devices with their start and end apart: 8, of which 6 were waited for; matrix products, arithmetic and copies ran while one was open for 16% of the time, Pallas kernels for 0%

commit v1 on v0

v1 whole, which is shorter than its diff:
```python
import functools

import jax
import jax.numpy as jnp
from jax import lax
from jax.experimental import pallas as pl
from jax.experimental.pallas import tpu as pltpu
from jax.sharding import PartitionSpec as P

AXIS_NAME = "fsdp"
NUM_DEV = 32
PLANE = 8
NUM_PLANES = 4
HOT_ROWS = 512
HOT_BLOCK = HOT_ROWS // NUM_DEV
ROW_GROUP = 8
CLASSES = ((0, 2, 5, 0), (2, 4, 3, 10), (4, 8, 2, 16), (8, 32, 1, 24))
SEND_GROUPS = 5
RECV_GROUPS = 48
PLANE_GROUPS = (21, 4, 3, 3)
PLANE_FIRST = (0, 21, 25, 28)
PLANE_TOTAL = 31
MESH = pl.DeviceIdType.MESH
ANY = pl.BlockSpec(memory_space=pl.ANY)
BF16_MAX = 3.3895313892515355e38


def owner_class(owner):
    for first, last, groups, start in CLASSES:
        if first <= owner < last:
            return groups, start + (owner - first) * groups


def remote(src, dst, send_sem, recv_sem, dev):
    return pltpu.make_async_remote_copy(src_ref=src, dst_ref=dst, send_sem=send_sem, recv_sem=recv_sem,
                                        device_id=(dev,), device_id_type=MESH)


def spread_kernel(tok_ref, gain_ref, tok_out, gain_out, send_sems, recv_sems, own_sems):
    me = lax.axis_index(AXIS_NAME)
    own = [pltpu.make_async_copy(tok_ref, tok_out.at[me], own_sems.at[0]),
           pltpu.make_async_copy(gain_ref, gain_out.at[me], own_sems.at[1])]
    for copy in own:
        copy.start()
    copies = []
    for step in range(1, NUM_DEV):
        dev = lax.rem(me + step, NUM_DEV)
        copies.append(remote(tok_ref, tok_out.at[me], send_sems.at[0, step], recv_sems.at[0, step], dev))
        copies.append(remote(gain_ref, gain_out.at[me], send_sems.at[1, step], recv_sems.at[1, step], dev))
    for copy in copies:
        copy.start()
    for step in range(1, NUM_DEV):
        src = lax.rem(me + NUM_DEV - step, NUM_DEV)
        remote(tok_ref, tok_out.at[src], send_sems.at[0, step], recv_sems.at[0, step], src).wait()
        remote(gain_ref, gain_out.at[src], send_sems.at[1, step], recv_sems.at[1, step], src).wait()
    for copy in own:
        copy.wait()


def rows_kernel(hot_ref, cold_ref, hot_out, cold_out, send_sems, recv_sems, hot_send, hot_recv,
                z_send, z_recv, p_send, p_recv, c_send, c_recv):
    me = lax.axis_index(AXIS_NAME)
    pos = lax.rem(me, PLANE)
    plane = me // PLANE
    core = lax.rem(me, 2)

    @pl.when(me == 0)
    def _():
        for dev in range(1, NUM_DEV):
            remote(hot_ref.at[dev], hot_out.at[dev], hot_send.at[dev], hot_recv, dev).start()
        pltpu.make_async_copy(hot_ref.at[0], hot_out.at[0], hot_recv).start()

    for first, last, groups, start in CLASSES:
        @pl.when((me >= first) & (me < last))
        def _():
            base = start + (me - first) * groups
            src_rows, dst_rows = pl.ds(0, groups), pl.ds(base, groups)
            pltpu.make_async_copy(cold_ref.at[me, src_rows], cold_out.at[dst_rows], recv_sems.at[me]).start()
            for step in range(1, NUM_DEV):
                dev = lax.rem(me + step, NUM_DEV)
                remote(cold_ref.at[dev, src_rows], cold_out.at[dst_rows], send_sems.at[step], recv_sems.at[me], dev).start()

    pltpu.make_async_copy(hot_ref.at[me], hot_out.at[me], hot_recv).wait()
    along = []
    for step in range(1, NUM_PLANES):
        dev = lax.rem(me + step * PLANE, NUM_DEV)
        along.append(remote(hot_out.at[me], hot_out.at[me], z_send.at[step], z_recv.at[step], dev))
    for copy in along:
        copy.start()
    for step in range(1, NUM_PLANES):
        src = lax.rem(me + NUM_DEV - step * PLANE, NUM_DEV)
        remote(hot_out.at[src], hot_out.at[src], z_send.at[step], z_recv.at[step], src).wait_recv()
    across = []
    for step in range(1, 4):
        dev = plane * PLANE + lax.rem(pos + 2 * step, PLANE)
        src = lax.rem(pos + PLANE - 2 * step, PLANE)
        for z in range(NUM_PLANES):
            block = hot_out.at[z * PLANE + pos]
            across.append((remote(block, block, p_send.at[step, z], p_recv.at[step, z], dev), z * PLANE + src, step, z))
    for copy, _, _, _ in across:
        copy.start()
    for _, src, step, z in across:
        block = hot_out.at[src]
        remote(block, block, p_send.at[step, z], p_recv.at[step, z], me).wait_recv()
    partner = me + 1 - 2 * core
    mine = []
    for k in range(NUM_DEV // 2):
        block = hot_out.at[2 * k + core]
        mine.append(remote(block, block, c_send.at[k], c_recv.at[k], partner))
    for copy in mine:
        copy.start()
    for k in range(NUM_DEV // 2):
        block = hot_out.at[2 * k + 1 - core]
        remote(block, block, c_send.at[k], c_recv.at[k], partner).wait_recv()

    for owner in range(NUM_DEV):
        groups, base = owner_class(owner)
        rows = cold_out.at[pl.ds(base, groups)]
        pltpu.make_async_copy(rows, rows, recv_sems.at[owner]).wait()
    for copy in along:
        copy.wait_send()
    for copy, _, _, _ in across:
        copy.wait_send()
    for copy in mine:
        copy.wait_send()
    for first, last, groups, start in CLASSES:
        @pl.when((me >= first) & (me < last))
        def _():
            rows = cold_ref.at[0, pl.ds(0, groups)]
            for step in range(1, NUM_DEV):
                pltpu.make_async_copy(rows, rows, send_sems.at[step]).wait()

    @pl.when(me == 0)
    def _():
        for dev in range(1, NUM_DEV):
            pltpu.make_async_copy(hot_ref.at[dev], hot_ref.at[dev], hot_send.at[dev]).wait()


def plane_kernel(src_ref, out_ref, send_sems, recv_sems):
    me = lax.axis_index(AXIS_NAME)
    pos = lax.rem(me, PLANE)
    base = me - pos
    own = pltpu.make_async_copy(src_ref.at[pos], out_ref.at[pos], recv_sems.at[0])
    own.start()
    copies = []
    for step in range(1, PLANE):
        peer = lax.rem(pos + step, PLANE)
        copies.append(remote(src_ref.at[peer], out_ref.at[pos], send_sems.at[step], recv_sems.at[step], base + peer))
    for copy in copies:
        copy.start()
    for step in range(1, PLANE):
        peer = lax.rem(pos + PLANE - step, PLANE)
        remote(src_ref.at[peer], out_ref.at[peer], send_sems.at[step], recv_sems.at[step], base + peer).wait()
    own.wait()


def owners_kernel(src_ref, out_ref, send_sems, recv_sems):
    me = lax.axis_index(AXIS_NAME)
    pos = lax.rem(me, PLANE)
    plane = me // PLANE
    for dst, (groups, first) in enumerate(zip(PLANE_GROUPS, PLANE_FIRST)):
        rows, into = src_ref.at[pl.ds(first, groups)], out_ref.at[plane, pl.ds(0, groups)]

        @pl.when(plane == dst)
        def _():
            pltpu.make_async_copy(rows, into, recv_sems.at[plane]).start()

        @pl.when(plane != dst)
        def _():
            remote(rows, into, send_sems.at[dst], recv_sems.at[plane], dst * PLANE + pos).start()

    for dst, (groups, first) in enumerate(zip(PLANE_GROUPS, PLANE_FIRST)):
        @pl.when(plane == dst)
        def _():
            for src in range(NUM_PLANES):
                into = out_ref.at[src, pl.ds(0, groups)]
                pltpu.make_async_copy(into, into, recv_sems.at[src]).wait()

        @pl.when(plane != dst)
        def _():
            rows = src_ref.at[pl.ds(first, groups)]
            pltpu.make_async_copy(rows, rows, send_sems.at[dst]).wait()


def collect_kernel(hot_ref, gain_ref, hot_out, gain_out, hot_send, hot_recv, send_sems, recv_sems, own_sem):
    me = lax.axis_index(AXIS_NAME)

    @pl.when(me == 0)
    def _():
        pltpu.make_async_copy(hot_ref, hot_out.at[me], hot_recv.at[0]).start()

    @pl.when(me != 0)
    def _():
        remote(hot_ref, hot_out.at[me], hot_send, hot_recv.at[me], 0).start()

    own = pltpu.make_async_copy(gain_ref.at[me], gain_out.at[me], own_sem)
    own.start()
    copies = []
    for step in range(1, NUM_DEV):
        dev = lax.rem(me + step, NUM_DEV)
        copies.append(remote(gain_ref.at[dev], gain_out.at[me], send_sems.at[step], recv_sems.at[step], dev))
    for copy in copies:
        copy.start()
    for step in range(1, NUM_DEV):
        src = lax.rem(me + NUM_DEV - step, NUM_DEV)
        remote(gain_ref.at[src], gain_out.at[src], send_sems.at[step], recv_sems.at[step], src).wait()
    own.wait()

    @pl.when(me == 0)
    def _():
        for src in range(NUM_DEV):
            pltpu.make_async_copy(hot_ref, hot_out.at[src], hot_recv.at[src]).wait()

    @pl.when(me != 0)
    def _():
        pltpu.make_async_copy(hot_ref, hot_ref, hot_send).wait()


def exchange(kernel, outs, sems, *args):
    return pl.pallas_call(
        kernel, out_shape=[jax.ShapeDtypeStruct(*out) for out in outs],
        in_specs=[ANY] * len(args), out_specs=[ANY] * len(outs),
        scratch_shapes=[pltpu.SemaphoreType.DMA(shape) if shape else pltpu.SemaphoreType.DMA for shape in sems],
        compiler_params=pltpu.CompilerParams(has_side_effects=True))(*args)


def split3(value):
    def top(v):
        return jnp.clip(lax.reduce_precision(v, 8, 7), -BF16_MAX, BF16_MAX)
    high = top(value)
    rest = value - high
    mid = top(rest)
    return [part.astype(jnp.bfloat16) for part in (high, mid, rest - mid)]


def ranks(mask):
    n = mask.shape[-1]
    lower = (jnp.arange(n)[:, None] < jnp.arange(n)[None, :]).astype(jnp.bfloat16)
    return jnp.dot(mask.astype(jnp.bfloat16), lower, preferred_element_type=jnp.float32).astype(jnp.int32)


def dot_rows(a, b):
    return lax.dot_general(a, b, (((1,), (1,)), ((), ())), preferred_element_type=jnp.float32)


def dot_tokens(a, b):
    return lax.dot_general(a, b, (((0,), (0,)), ((), ())), preferred_element_type=jnp.float32)


def norm_forward(x_rows):
    inv_rms = lax.rsqrt(jnp.mean(x_rows * x_rows, axis=-1, keepdims=True) + 1e-5)
    return inv_rms, x_rows * inv_rms


def norm_backward(d_normed, h_rows, inv_rms, gain_full):
    u_rows = d_normed * gain_full
    return inv_rms * (u_rows - h_rows * jnp.mean(u_rows * h_rows, axis=-1, keepdims=True))


def solution(mesh):
    ring = [(d, (d + 1) % NUM_DEV) for d in range(NUM_DEV)]
    plane_groups = [[z * PLANE + p for p in range(PLANE)] for z in range(NUM_PLANES)]
    column_groups = [[z * PLANE + p for z in range(NUM_PLANES)] for p in range(PLANE)]
    caps = jnp.array([owner_class(d)[0] * ROW_GROUP for d in range(NUM_DEV)], jnp.int32)
    starts = jnp.array([HOT_ROWS + owner_class(d)[1] * ROW_GROUP for d in range(NUM_DEV)], jnp.int32)
    plane_caps = jnp.array([g * ROW_GROUP for g in PLANE_GROUPS], jnp.int32)
    slot_plane = jnp.array([z for z, g in enumerate(PLANE_GROUPS) for _ in range(g * ROW_GROUP)], jnp.int32)
    slot_rank = jnp.array([c for g in PLANE_GROUPS for c in range(g * ROW_GROUP)], jnp.int32)

    def local_step(tokens, embed_shard, gain_shard, wq_shard, wk_shard, wv_shard, d_query, d_key, d_value):
        vocab_local, width = embed_shard.shape
        seq = tokens.shape[1]
        q_width, kv_width = wq_shard.shape[1], wk_shard.shape[1]
        out_width = q_width + 2 * kv_width
        block = width // NUM_DEV
        me = lax.axis_index(AXIS_NAME)
        pos, plane = me % PLANE, me // PLANE
        bf16, f32 = jnp.bfloat16, jnp.float32

        cot_mine = jnp.concatenate([d_query[0], d_key[0], d_value[0]], axis=1)
        cot_plane = lax.all_gather(cot_mine, AXIS_NAME, axis=0, tiled=True, axis_index_groups=plane_groups)
        w_mine = jnp.concatenate([wq_shard.astype(bf16), wk_shard.astype(bf16), wv_shard.astype(bf16)], axis=1)
        w_full = lax.all_gather(w_mine, AXIS_NAME, axis=0, tiled=True)

        gain_row = jnp.pad(gain_shard, (0, 128 - block))[None]
        all_tokens, gain_rows = exchange(
            spread_kernel, [((NUM_DEV, 1, seq), jnp.int32), ((NUM_DEV, 1, 128), f32)],
            [(2, NUM_DEV), (2, NUM_DEV), (2,)], tokens, gain_row)
        all_tokens = all_tokens[:, 0]
        gain_full = gain_rows[:, 0, :block].reshape(1, width)

        all_owner = all_tokens // vocab_local
        all_cold = all_tokens >= HOT_ROWS
        counts = jnp.sum((all_owner[:, :, None] == jnp.arange(NUM_DEV)) & all_cold[:, :, None], axis=1, dtype=jnp.int32)
        plane_counts = counts.reshape(NUM_PLANES, PLANE, NUM_PLANES, PLANE).sum(1)
        rows_fit = jnp.all(counts <= caps[None])
        cots_fit = jnp.all(plane_counts <= plane_caps[None, :, None])

        to_mine = (all_owner == me) & all_cold
        to_rank = ranks(to_mine)
        slots = jnp.arange(SEND_GROUPS * ROW_GROUP)
        picks = (to_rank[:, None, :] == slots[None, :, None]) & to_mine[:, None, :]
        local_ids = all_tokens - me * vocab_local
        pick_ids = jnp.sum(jnp.where(picks, local_ids[:, None, :], 0), axis=2)
        send_rows = embed_shard[pick_ids.reshape(-1)].astype(bf16)
        hot_mine = embed_shard[:HOT_ROWS].astype(bf16)
        hot_rows, cold_rows = exchange(
            rows_kernel,
            [((NUM_DEV, HOT_BLOCK, width), bf16), ((RECV_GROUPS, ROW_GROUP, width), bf16)],
            [(NUM_DEV,), (NUM_DEV,), (NUM_DEV,), (), (4,), (4,), (4, 4), (4, 4), (16,), (16,)],
            hot_mine.reshape(NUM_DEV, HOT_BLOCK, width),
            send_rows.reshape(NUM_DEV, SEND_GROUPS, ROW_GROUP, width))

        my_ids = tokens[0]
        my_owner = my_ids // vocab_local
        my_cold = my_ids >= HOT_ROWS
        before = jnp.arange(seq)[None, :] < jnp.arange(seq)[:, None]
        my_rank = jnp.sum(before & my_cold[None, :] & (my_owner[None, :] == my_owner[:, None]), axis=1, dtype=jnp.int32)

        def fetched_rows(_):
            start = jnp.sum(jnp.where(my_owner[:, None] == jnp.arange(NUM_DEV), starts[None], 0), axis=1)
            place = jnp.where(my_cold, start + my_rank, my_ids)
            table = jnp.concatenate([hot_rows.reshape(HOT_ROWS, width), cold_rows.reshape(-1, width)])
            select = (place[:, None] == jnp.arange(table.shape[0])).astype(bf16)
            return jnp.dot(select, table, preferred_element_type=f32)

        def ring_rows(_):
            def hop(_, carry):
                ids, rows = carry
                mine = ids // vocab_local == me
                own = embed_shard[jnp.where(mine, ids - me * vocab_local, 0)].astype(bf16)
                rows = jnp.where(mine[:, None], own, rows)
                return lax.ppermute(ids, AXIS_NAME, ring), lax.ppermute(rows, AXIS_NAME, ring)
            return lax.fori_loop(0, NUM_DEV, hop, (my_ids, jnp.zeros((seq, width), bf16)))[1].astype(f32)

        x_rows = lax.cond(rows_fit, fetched_rows, ring_rows, None)
        inv_rms, h_rows = norm_forward(x_rows)
        normed = (h_rows * gain_full).astype(bf16)

        slices = normed.reshape(seq, NUM_PLANES, PLANE, block).transpose(2, 0, 1, 3).reshape(PLANE, seq, NUM_PLANES * block)
        n_plane, = exchange(plane_kernel, [((PLANE, seq, NUM_PLANES * block), bf16)], [(PLANE,), (PLANE,)], slices)
        n_plane = n_plane.reshape(PLANE * seq, NUM_PLANES * block)

        plane_tokens = lax.dynamic_slice_in_dim(all_tokens, plane * PLANE, PLANE, 0).reshape(PLANE * seq)
        z_ids, block_ids = jnp.arange(NUM_PLANES * HOT_BLOCK) // HOT_BLOCK, jnp.arange(NUM_PLANES * HOT_BLOCK) % HOT_BLOCK
        hot_ids = (z_ids * PLANE + pos) * HOT_BLOCK + block_ids
        hot_select = (plane_tokens[:, None] == hot_ids[None, :]).astype(bf16)
        d_w_part = dot_tokens(n_plane, cot_plane).reshape(NUM_PLANES, block, out_width)
        hot_part = dot_tokens(hot_select, cot_plane).reshape(NUM_PLANES, HOT_BLOCK, out_width)
        parts = jnp.concatenate([d_w_part, hot_part], axis=1).reshape(-1, out_width)
        summed = lax.psum_scatter(parts, AXIS_NAME, scatter_dimension=0, tiled=True, axis_index_groups=column_groups)
        d_w, hot_cot = summed[:block], summed[block:]

        plane_owner = plane_tokens // vocab_local
        here = (plane_owner % PLANE == pos) & (plane_tokens >= HOT_ROWS)
        to_plane = (plane_owner // PLANE)[None] == jnp.arange(NUM_PLANES)[:, None]
        plane_rank = jnp.sum(jnp.where(to_plane, ranks(to_plane & here), 0), axis=0)
        pack = (here & (plane_owner // PLANE == slot_plane[:, None]) & (plane_rank == slot_rank[:, None])).astype(bf16)
        packed = jnp.dot(pack, cot_plane, preferred_element_type=f32).astype(bf16)
        got, = exchange(owners_kernel, [((NUM_PLANES, PLANE_GROUPS[0], ROW_GROUP, out_width), bf16)],
                        [(NUM_PLANES,), (NUM_PLANES,)], packed.reshape(PLANE_TOTAL, ROW_GROUP, out_width))

        from_mine = to_mine.reshape(NUM_PLANES, PLANE * seq)
        from_rank = ranks(from_mine)
        from_slots = jnp.arange(PLANE_GROUPS[0] * ROW_GROUP)
        from_picks = (from_rank[:, None, :] == from_slots[None, :, None]) & from_mine[:, None, :]
        got_ids = jnp.sum(jnp.where(from_picks, local_ids.reshape(NUM_PLANES, 1, -1), 0), axis=2).reshape(-1)
        limit = jnp.sum(jnp.where(plane == jnp.arange(NUM_PLANES), plane_caps, 0))
        got_valid = ((from_slots[None] < jnp.sum(from_mine, axis=1, dtype=jnp.int32)[:, None])
                     & (from_slots < limit)[None]).reshape(-1, 1)
        got_inv, got_h = norm_forward(embed_shard[got_ids].astype(bf16).astype(f32))
        got_dn = jnp.where(got_valid, dot_rows(got.reshape(-1, out_width), w_full), 0.0)
        got_dx = norm_backward(got_dn, got_h, got_inv, gain_full)

        my_hot = lax.dynamic_index_in_dim(hot_rows, me, 0, keepdims=False).astype(f32)
        hot_inv, hot_h = norm_forward(my_hot)
        hot_dn3 = dot_rows(jnp.concatenate(split3(hot_cot)), w_full).reshape(3, HOT_BLOCK, width)
        hot_dn = hot_dn3[0] + hot_dn3[1] + hot_dn3[2]
        hot_dx = norm_backward(hot_dn, hot_h, hot_inv, gain_full)

        gain_part = jnp.sum(got_dn * got_h, axis=0) + jnp.sum(hot_dn * hot_h, axis=0)
        gain_part = jnp.pad(gain_part.reshape(NUM_DEV, 1, block), ((0, 0), (0, 0), (0, 128 - block)))
        hot_back, gain_back = exchange(
            collect_kernel, [((NUM_DEV, HOT_BLOCK, width), f32), ((NUM_DEV, 1, 128), f32)],
            [(), (NUM_DEV,), (NUM_DEV,), (NUM_DEV,), ()], hot_dx, gain_part)

        place = ((jnp.arange(vocab_local)[:, None] == got_ids[None, :]) & got_valid[:, 0][None]).astype(bf16)
        cold_grad = jnp.dot(jnp.concatenate([place] * 3, axis=1), jnp.concatenate(split3(got_dx)), preferred_element_type=f32)

        def owner_sums(_):
            top = jnp.where(me == 0, hot_back.reshape(HOT_ROWS, width), cold_grad[:HOT_ROWS])
            return jnp.concatenate([top, cold_grad[HOT_ROWS:]]), jnp.sum(gain_back[:, 0, :block], axis=0)

        def ring_sums(_):
            d_normed = dot_rows(cot_mine, w_full)
            d_gain = lax.psum(jnp.sum(d_normed * h_rows, axis=0), AXIS_NAME)
            d_x = norm_backward(d_normed, h_rows, inv_rms, gain_full)

            def hop(_, carry):
                ids, rows, total = carry
                mine = ids // vocab_local == me
                total = total.at[jnp.where(mine, ids - me * vocab_local, vocab_local)].add(rows, mode="drop")
                return lax.ppermute(ids, AXIS_NAME, ring), lax.ppermute(rows, AXIS_NAME, ring), total
            total = lax.fori_loop(0, NUM_DEV, hop, (my_ids, d_x, jnp.zeros(embed_shard.shape, f32)))[2]
            return total, lax.dynamic_slice_in_dim(d_gain, me * block, block)

        d_embed, d_norm_gain = lax.cond(cots_fit, owner_sums, ring_sums, None)

        proj = jnp.dot(normed, w_full, preferred_element_type=f32).astype(bf16)[None]
        return (proj[..., :q_width], proj[..., q_width:q_width + kv_width], proj[..., q_width + kv_width:], d_embed, d_norm_gain,
                d_w[:, :q_width], d_w[:, q_width:q_width + kv_width], d_w[:, q_width + kv_width:])

    row_spec = P(AXIS_NAME, None)
    act_spec = P(AXIS_NAME, None, None)
    vec_spec = P(AXIS_NAME)
    return jax.shard_map(local_step, mesh=mesh,
                         in_specs=(row_spec, row_spec, vec_spec, row_spec, row_spec, row_spec, act_spec, act_spec, act_spec),
                         out_specs=(act_spec, act_spec, act_spec, row_spec, vec_spec, row_spec, row_spec, row_spec),
                         check_vma=False)
```

time: 1390 us -> 492 us (0.35)
  waiting for transfers between devices: 1010 us -> 27.1 us
  Pallas kernels: 0 us -> 293 us
  blocking collectives: 129 us -> 0 us
  other arithmetic: 136 us -> 35.2 us
  matrix products: 33.1 us -> 60.6 us
  local copies, waits for them, and re-layouts: 66.4 us -> 51.4 us
    reduce_scatter x4 -> x1, waiting for transfers between devices: 660 us -> 27 us  [local_step(): lax.psum_scatter(parts, AXIS_NAME, scatter_dimension=0, tiled=True, axis_...]
    all_gather x4 -> x2, waiting for transfers between devices: 354 us -> 0.04 us  [the longest x1 0.02 us: local_step(): lax.all_gather(cot_mine, AXIS_NAME, axis=0, tiled=True, axis_index_groups...]
    pallas_call x0 -> x5, Pallas kernels: none -> 293 us  [exchange(): pl.pallas_call(kernel, out_shape=[jax.ShapeDtypeStruct(*out) for out in o...]
    scatter-add x1 -> x0, other arithmetic: 106 us -> none  [local_step(): jnp.zeros(embed_shard.shape, jnp.float32).at[scatter_ids]]
    unnamed x2 -> x0, blocking collectives: 85.9 us -> none
    all_gather x1 -> x0, blocking collectives: 43.4 us -> none  [local_step(): all_tokens = lax.all_gather(tokens, AXIS_NAME, axis=0, tiled=True)]
    gather x1 -> x2, local copies, waits for them, and re-layouts: 64.7 us -> 24.5 us  [the longest x1 14.1 us: local_step(): send_rows = embed_shard[pick_ids.reshape(-1)].astype(bf16)]
    dot_general x9 -> x11, matrix products: 33.1 us -> 60.6 us  [the longest x2 17 us: dot_rows(): lax.dot_general(a, b, (((1,), (1,)), ((), ())), preferred_element_type=jn...]
  transfers between devices with their start and end apart: 8 -> 3, of which waited for: 6 -> 1; matrix products, arithmetic and copies ran while one was open for 16% -> 24% of each run, Pallas kernels for 0% -> 56%
where the time goes in v1:
time: 492 us; the launch traced here: 483 us
  Pallas kernels  293 us (60%)
  matrix products  60.6 us (12%)
  local copies, waits for them, and re-layouts  51.4 us (10%)
  other arithmetic  35.2 us (7%)
  waiting for transfers between devices  27.1 us (6%)
  between operations  15.8 us (3%)
    pallas_call x5, Pallas kernels, exchange(): pl.pallas_call(kernel, out_shape=[jax.ShapeDtypeStruct(*out) for out in o...  293 us
    reduce_scatter x1, waiting for transfers between devices, local_step(): lax.psum_scatter(parts, AXIS_NAME, scatter_dimension=0, tiled=True, axis_...  27 us
    dot_general x2, matrix products, dot_rows(): lax.dot_general(a, b, (((1,), (1,)), ((), ())), preferred_element_type=jn...  17 us
    gather x1, local copies, waits for them, and re-layouts, local_step(): send_rows = embed_shard[pick_ids.reshape(-1)].astype(bf16)  14.1 us
    dot_general x1, matrix products, local_step(): jnp.dot(jnp.concatenate([place] * 3, axis=1), jnp.concatenate(split3(got_...  11 us
    dot_general x2, matrix products, dot_tokens(): lax.dot_general(a, b, (((0,), (0,)), ((), ())), preferred_element_type=jn...  10.9 us
    gather x1, local copies, waits for them, and re-layouts, local_step(): got_inv, got_h = norm_forward(embed_shard[got_ids].astype(bf16).astype(f32))  10.3 us
  transfers between devices with their start and end apart: 3, of which 1 were waited for; matrix products, arithmetic and copies ran while one was open for 24% of the time, Pallas kernels for 56%

profile of v1, /device:TPU:0, one launch (start us, length us, event | category | flops | bytes accessed | tf_op | source)
XLA Modules:
  0.0 483.2 jit_solution(6323082168899813940)
XLA Ops:
  8.0 2.6 pad_maximum_fusion.2
  12.1 15.7 %shard_map.198 = (s32[32,1,256]{2,1,0:T(1,128)}, f32[32,1,128]{2,1,0:T(1,128)}) custom-call(s32[1,256]{1,0:T(1,128)S(1)} %copy.105.tok_ref, f32[1,128]{1,0:T(1,128)} %pad_bitcast_fusion.gain_ref), custom_call_target="tpu_custom_call" | custom-call | tf_op jit(solution)/shard_map/pallas_call | solution.py:220
  35.1 3.9 slice.97
  39.1 10.3 %gather_fusion.2 = bf16[672,2048]{1,0:T(8,128)(2,1)} fusion(f32[1000,2048]{1,0:T(8,128)} %param.23, s32[1024]{0:T(1024)S(1)} %pad_clamp_fusion.2), kind=kCustom, calls=%fused_computation.2 | custom fusion | bytes 5507712 | tf_op jit(solution)/shard_map/gather | solution.py:371
  50.1 5.8 %concatenate.31 = pred[1000,2016]{1,0:T(8,128)(4,1)} concatenate(pred[1000,672]{1,0:T(8,128)(4,1)S(1)} %fusion.31, pred[1000,672]{1,0:T(8,128)(4,1)S(1)} %fusion.31, pred[1000,672]{1,0:T(8,128)(4,1)S(1)} %fusion.31), dimensions={1} | concatenate | bytes 4032000 | tf_op jit(solution)/shard_map/concatenate | solution.py:388
  56.9 14.1 %gather_fusion.1 = bf16[1280,2048]{1,0:T(8,128)(2,1)} fusion(f32[1000,2048]{1,0:T(8,128)} %param.23, s32[2048]{0:T(1024)S(1)} %pad_clamp_fusion.1), kind=kCustom, calls=%fused_computation.1 | custom fusion | bytes 10490880 | tf_op jit(solution)/shard_map/gather | solution.py:305
  73.1 160.3 %shard_map.199 = (bf16[32,16,2048]{2,1,0:T(8,128)(2,1)}, bf16[48,8,2048]{2,1,0:T(8,128)(2,1)}) custom-call(bf16[32,16,2048]{2,1,0:T(8,128)(2,1)} %bitcast.72, bf16[32,5,8,2048]{3,2,1,0:T(8,128)(2,1)} %bitcast.69), custom_call_target="tpu_custom_call" | custom-call | tf_op jit(solution)/shard_map/pallas_call | solution.py:220
  233.6 5.7 %conditional.2 = (f32[256,2048]{1,0:T(8,128)}, f32[256,1]{0,1:T(1,128)S(1)}) conditional(s32[]{:T(128)} %convert_element_type.105, (s32[]{:T(128)}, f32[1000,2048]{1,0:T(8,128)}, s32[256]{0:T(256)S(1)}) %tuple.118, (s32[256]{0:T(256)S(1)}, s32[256]{0:T(256)S(1)}, s32[256]{0:T(256)S(1)}, (), s32[256,256]{1,0:T(8,128)S(1)}, ...), branch_computations={%region_3.7_spmd, %region_7.11_spmd} | conditional | flops 948233984 | bytes 25937668 | solution.py:336
  234.6 4.7 multiply_reduce_fusion
  239.3 1.9 copy.43
  241.2 1.7 multiply_convert_fusion
  245.3 28.6 %shard_map.200 = bf16[8,256,256]{2,1,0:T(8,128)(2,1)} custom-call(bf16[8,256,256]{2,1,0:T(8,128)(2,1)} %copy.46.src_ref), custom_call_target="tpu_custom_call" | custom-call | tf_op jit(solution)/shard_map/pallas_call | solution.py:220
  273.9 2.4 copy.47
  280.2 7.9 %fusion.30.src_ref = bf16[31,8,2560]{2,1,0:T(8,128)(2,1)} fusion(bf16[2048,2560]{1,0:T(8,128)(2,1)} %all-gather.5.cloned.1.call-done, s32[2048]{0:T(1024)S(1)} %fusion.40, s32[2048]{0:T(1024)S(1)} %add_select_fusion.2, s32[248]{0:T(256)S(1)} %copy-done.16, s32[248]{0:T(256)S(1)} %copy-done.15, pred[2048]{0:T(1024)(128)(4,1)S(1)} %fusion.84), kind=kOutput, calls=%fused_computation.66 | convolution fusion | flops 2603134976 | bytes 11775936 | tf_op jit(solution)/shard_map/dot_general | solution.py:359
  288.1 63.8 %shard_map.201 = bf16[4,21,8,2560]{3,2,1,0:T(8,128)(2,1)} custom-call(bf16[31,8,2560]{2,1,0:T(8,128)(2,1)} %fusion.30.src_ref), custom_call_target="tpu_custom_call" | custom-call | tf_op jit(solution)/shard_map/pallas_call | solution.py:220
  352.0 5.3 %fusion.42 = f32[64,2560]{1,0:T(8,128)S(1)} fusion(bf16[2048,2560]{1,0:T(8,128)(2,1)} %all-gather.5.cloned.1.call-done, s32[64]{0:T(128)S(1)} %fusion.89, s32[2048]{0:T(1024)S(1)} %bitcast.81), kind=kOutput, calls=%fused_computation.88 | convolution fusion | flops 671219712 | bytes 11149568 | tf_op jit(solution)/shard_map/dot_general | solution.py:247
  357.3 5.6 %fusion.9 = f32[4,64,2560]{2,1,0:T(8,128)S(1)} fusion(bf16[4,64,2048]{2,1,0:T(8,128)(2,1)S(1)} %bitcast.78, bf16[2048,2560]{1,0:T(8,128)(2,1)} %all-gather.5.cloned.1.call-done), kind=kOutput, calls=%fused_computation.35 | convolution fusion | flops 2684354560 | bytes 14155776 | tf_op jit(solution)/shard_map/dot_general | solution.py:247
  362.9 1.9 pad_maximum_fusion.1
  364.9 7.3 %fusion.29 = bf16[1,256,2560]{2,1,0:T(8,128)(2,1)S(1)} fusion(bf16[256,2048]{0,1:T(8,128)(2,1)} %copy-done.2, bf16[2048,2560]{1,0:T(8,128)(2,1)} %all-gather.3.cloned.1.call-done), kind=kOutput, calls=%fused_computation.65 | convolution fusion | flops 2685009920 | bytes 12845056 | tf_op jit(solution)/shard_map/dot_general | solution.py:409
  373.3 9.8 %fusion.21 = (f32[672]{0:T(1024)S(1)}, f32[2048]{0:T(1024)S(1)}, f32[672,2048]{1,0:T(8,128)S(1)}) fusion(bf16[672,2048]{1,0:T(8,128)(2,1)S(1)} %copy-done.1, f32[2048]{0:T(1024)S(1)} %mul.180, f32[672]{0:T(1024)S(1)} %add_rsqrt_fusion, pred[672]{0:T(1024)(128)(4,1)S(1)} %and.246, bf16[672,2560]{1,0:T(8,128)(2,1)} %bitcast.75, bf16[2048,2560]{1,0:T(8,128)(2,1)S(1)} %copy-done), kind=kOutput, calls=%fused_computation.49 | convolution fusion | flops 7057438208 | bytes 22206368 | tf_op jit(solution)/shard_map/dot_general | solution.py:243
  383.9 2.2 fusion.27
  386.1 1.6 fusion.25
  387.6 11.0 %fusion.11 = f32[1000,2048]{1,0:T(8,128)} fusion(pred[1000,2016]{1,0:T(8,128)(4,1)S(1)} %copy-done.4, bf16[672,2048]{1,0:T(8,128)(2,1)S(1)} %get-tuple-element.326, bf16[672,2048]{1,0:T(8,128)(2,1)S(1)} %get-tuple-element.325, bf16[672,2048]{1,0:T(8,128)(2,1)S(1)} %get-tuple-element.310), kind=kOutput, calls=%fused_computation.37 | convolution fusion | flops 8282308608 | bytes 18465536 | tf_op jit(solution)/shard_map/dot_general | solution.py:388
  398.6 27.0 %reduce-scatter.2.cloned.1.call-done = f32[80,2560]{1,0:T(8,128)} async-done(((f32[320,2560]{1,0:T(8,128)}), f32[80,2560]{1,0:T(8,128)}) %reduce-scatter.2.cloned.1.call-update) | async-done | bytes 819216 | tf_op jit(solution)/shard_map/reduce_scatter | solution.py:351
  426.5 7.2 %fusion.54 = f32[48,2048]{1,0:T(8,128)S(1)} fusion(bf16[2048,2560]{1,0:T(8,128)(2,1)} %all-gather.3.cloned.1.call-done, bf16[16,2560]{1,0:T(8,128)(2,1)S(1)} %get-tuple-element.332, bf16[16,2560]{1,0:T(8,128)(2,1)S(1)} %get-tuple-element.333, bf16[16,2560]{1,0:T(8,128)(2,1)S(1)} %get-tuple-element.331), kind=kOutput, calls=%fused_computation.103 | convolution fusion | flops 504053760 | bytes 11124736 | tf_op jit(solution)/shard_map/dot_general | solution.py:243
  435.6 1.6 fusion.68.hot_ref
  437.1 24.5 %shard_map.202 = (f32[32,16,2048]{2,1,0:T(8,128)}, f32[32,1,128]{2,1,0:T(1,128)S(1)}) custom-call(f32[16,2048]{1,0:T(8,128)} %fusion.68.hot_ref, f32[32,1,128]{2,1,0:T(1,128)} %pad.9.gain_ref), custom_call_target="tpu_custom_call" | custom-call | tf_op jit(solution)/shard_map/pallas_call | solution.py:220
  461.7 11.4 %conditional.3 = (f32[1000,2048]{1,0:T(8,128)}, f32[64]{0:T(128)S(1)}) conditional(s32[]{:T(128)} %convert_element_type.115, (f32[256,1]{0,1:T(1,128)S(1)}, bf16[256,2560]{1,0:T(8,128)(2,1)S(1)}, bf16[2048,2560]{1,0:T(8,128)(2,1)}, f32[32,1,64]{2,1,0:T(1,128)S(1)}, f32[256,2048]{0,1:T(8,128)}, /*index=5*/s32[]{:T(128)}, ...), branch_computations={%region_25.32_spmd, %region_32.34_spmd} | conditional | flops 2689601024 | bytes 53631808 | solution.py:407
  461.7 4.4 bitcast_select_fusion
  466.1 2.6 slice.39
  468.7 4.3 pad_maximum_fusion
  473.1 1.9 slice.79
  (119 shorter events, 25.5 us)
Async XLA Ops:
  7.2 4.4 copy-start.13
  7.2 3.5 copy-start.7
  7.2 3.5 copy-start.8
  7.2 3.5 copy-start.9
  7.2 273.0 %all-gather.5.cloned.1.call-start = ((), (), s32[]{:S(2)}) async-start(), calls=%async_computation.2 | async-start | bytes 11796480 | tf_op jit(solution)/shard_map/all_gather | solution.py:281
  10.6 23.1 %copy-start.11 = (s32[4]{0:T(128)S(1)}, s32[4]{0:T(128)}, u32[]{:S(2)}) copy-start(s32[4]{0:T(128)} %constant.231.clone) | copy-start | bytes 52
  10.6 354.3 %all-gather.3.cloned.1.call-start = ((), (), s32[]{:S(2)}) async-start(), calls=%async_computation.1 | async-start | bytes 10813440 | tf_op jit(solution)/shard_map/all_gather | solution.py:283
  11.5 414.1 %reduce-scatter.2.cloned.1.call-start = ((), (), s32[]{:S(2)}) async-start(), calls=%async_computation.3 | async-start | bytes 4096000 | tf_op jit(solution)/shard_map/reduce_scatter | solution.py:351
  39.1 10.3 %copy-start.10 = (f32[32,1,128]{2,1,0:T(1,128)S(1)}, f32[32,1,128]{2,1,0:T(1,128)}, u32[]{:S(2)}) copy-start(f32[32,1,128]{2,1,0:T(1,128)} %get-tuple-element.255) | copy-start | bytes 49156
  49.4 6.5 %copy-start.6 = (s32[32,1,256]{2,1,0:T(1,128)S(1)}, s32[32,1,256]{2,1,0:T(1,128)}, u32[]{:S(2)}) copy-start(s32[32,1,256]{2,1,0:T(1,128)} %get-tuple-element.250) | copy-start | bytes 98308
  56.9 14.9 %copy-start.12 = (s32[32]{0:T(128)S(1)}, s32[32]{0:T(128)}, u32[]{:S(2)}) copy-start(s32[32]{0:T(128)} %constant.230.clone) | copy-start | bytes 388
  242.9 1.0 copy-start.2
  273.8 5.7 %copy-start.1 = (bf16[672,2048]{1,0:T(8,128)(2,1)S(1)}, bf16[672,2048]{1,0:T(8,128)(2,1)}, u32[]{:S(2)}) copy-start(bf16[672,2048]{1,0:T(8,128)(2,1)} %gather_fusion.2) | copy-start | bytes 8257540
  276.3 4.0 copy-start.15
  276.3 4.0 copy-start.16
  351.9 5.3 %copy-start.5 = (bf16[256,2048]{1,0:T(8,128)(2,1)S(1)}, bf16[256,2048]{1,0:T(8,128)(2,1)}, u32[]{:S(2)}) copy-start(bf16[256,2048]{1,0:T(8,128)(2,1)} %copy.47) | copy-start | bytes 3145732
  364.9 8.5 %copy-start = (bf16[2048,2560]{1,0:T(8,128)(2,1)S(1)}, bf16[2048,2560]{1,0:T(8,128)(2,1)}, u32[]{:S(2)}) copy-start(bf16[2048,2560]{1,0:T(8,128)(2,1)} %all-gather.3.cloned.1.call-done) | copy-start | bytes 31457284
  386.0 1.6 copy-start.4
  426.5 35.2 %copy-start.3 = (bf16[256,2560]{1,0:T(8,128)(2,1)S(1)}, bf16[256,2560]{1,0:T(8,128)(2,1)}, u32[]{:S(2)}) copy-start(bf16[256,2560]{1,0:T(8,128)(2,1)} %pad_maximum_fusion.2) | copy-start | bytes 3932164
  473.1 3.4 copy-start.14
Sparse Core Ops, SparseCore 0:
  10.7 66.0 all-gather.4
  80.2 135.8 all-gather.2
  365.0 60.5 reduce-scatter.1
